TPU v7x, 32 devices: a whole 2x2x4 slice. The times are simulated.
32 devices in a mesh: row: 4 (over y, x), col: 8 (over z, core).
Axes of the slice: x: 2, y: 2, z: 4, core: 2. Of those that a mesh axis runs over, the one named last changes fastest.
Arguments:
- features: bfloat16 [131072, 256], P(('row', 'col')), may hold values from -6 to 6
- send_rows: int32 [32, 32, 128], P(('row', 'col')), may hold values from 0 to 4095
- counts: int32 [32, 32], P(('row', 'col')), may hold values from 112 to 128, as said below
- tile_dst: int32 [32, 64], P(('row', 'col')), may hold values from 0 to 31
- tile_src: int32 [32, 64], P(('row', 'col')), may hold values from 0 to 63, each once within a row
- tiles: int32 [32, 64, 128, 128], P(('row', 'col')), may hold values 0 or 1
- w_self: bfloat16 [256, 256], replicated, may hold values from -0.375 to 0.375
- w_neigh: bfloat16 [256, 256], replicated, may hold values from -1.5 to 1.5
- bias: float32 [256], replicated, may hold values from -1 to 1
- cotangent: bfloat16 [131072, 256], P(('row', 'col')), may hold values from -6 to 6
Outputs:
- layer_out: bfloat16 [131072, 256], P(('row', 'col'))
- grad_features: float32 [131072, 256], P(('row', 'col'))
- grad_self: float32 [256, 256], replicated
- grad_neigh: float32 [256, 256], replicated
- grad_bias: float32 [256], replicated
Inputs may be any that keep to these rules, and one draw needn't show every extreme that they name: Every partition p has some q with counts[p, q] = 128.
All inputs are finite; a program needn't handle non-finite values. No bound on the sum of `tiles` on one device may be relied on, other than what follows from the above.
Results may differ from a plain program's by a relative error of at most 0.0051.
Values may be sent and summed in bfloat16 or wider, within the bound.
No kernel may reach another device: no remote copies, remote signals or barrier semaphores. Data moves between devices by JAX's collectives and lax.ppermute only.
A program may use at most 192 MiB of HBM per device.

v0:
```python
import jax
import jax.numpy as jnp
from jax import lax
from jax.sharding import PartitionSpec as P


def move_rows(block):
    return lax.all_to_all(block, ("row", "col"), split_axis=0, concat_axis=0, tiled=True)


def move_grads(block):
    return lax.all_to_all(block, ("row", "col"), split_axis=0, concat_axis=0, tiled=True)


def on_device(
    features, send_rows, counts, tile_dst, tile_src, tiles, w_self, w_neigh, bias, cotangent
):
    rows_own, width = features.shape
    peers = send_rows.shape[1]
    tile_rows = send_rows.shape[2]
    own_blocks = rows_own // tile_rows
    src_blocks = own_blocks + peers
    picks = send_rows[0]
    slots = jnp.arange(tile_rows, dtype=jnp.int32)
    keep = (slots[None, :] < counts[0][:, None]).reshape(-1)
    flat_picks = picks.reshape(-1)
    outgoing = jnp.take(features, flat_picks, axis=0) * keep[:, None].astype(jnp.bfloat16)
    arrived = move_rows(outgoing.reshape(peers, tile_rows, width))
    source = jnp.concatenate([features, arrived.reshape(peers * tile_rows, width)], 0)
    source = source.reshape(src_blocks, tile_rows, width)
    dst = tile_dst[0]
    src = tile_src[0]
    adj_int = tiles[0]
    adj = adj_int.astype(jnp.bfloat16)
    picked = jnp.take(source, src, axis=0)
    prod = jnp.einsum("tij,tjf->tif", adj, picked, preferred_element_type=jnp.float32)
    neigh = jax.ops.segment_sum(prod, dst, num_segments=own_blocks).reshape(rows_own, width)
    degree = jax.ops.segment_sum(
        jnp.sum(adj_int, axis=2).astype(jnp.float32), dst, num_segments=own_blocks
    ).reshape(rows_own)
    scale = 1.0 / (1.0 + degree)
    agg = (neigh * scale[:, None]).astype(jnp.bfloat16)
    pre = (
        jnp.dot(features, w_self, preferred_element_type=jnp.float32)
        + jnp.dot(agg, w_neigh, preferred_element_type=jnp.float32)
        + bias
    )
    sig = jax.nn.sigmoid(pre)
    layer_out = (pre * sig).astype(jnp.bfloat16)
    dpre = cotangent.astype(jnp.float32) * (sig * (1.0 + pre * (1.0 - sig)))
    dpre_b = dpre.astype(jnp.bfloat16)
    term_self = lax.dot_general(
        features, dpre_b, (((0,), (0,)), ((), ())), preferred_element_type=jnp.float32
    )
    term_neigh = lax.dot_general(
        agg, dpre_b, (((0,), (0,)), ((), ())), preferred_element_type=jnp.float32
    )
    term_bias = jnp.sum(dpre, axis=0)
    g_rows = lax.dot_general(
        dpre_b, w_neigh, (((1,), (1,)), ((), ())), preferred_element_type=jnp.float32
    )
    g_rows = (g_rows * scale[:, None]).astype(jnp.bfloat16)
    g_blocks = jnp.take(g_rows.reshape(own_blocks, tile_rows, width), dst, axis=0)
    back = jnp.einsum("tij,tif->tjf", adj, g_blocks, preferred_element_type=jnp.float32)
    back_sum = jax.ops.segment_sum(back, src, num_segments=src_blocks).reshape(
        src_blocks * tile_rows, width
    )
    back_b = back_sum[rows_own:].astype(jnp.bfloat16)
    returned = move_grads(back_b.reshape(peers, tile_rows, width))
    returned = returned.reshape(peers * tile_rows, width).astype(jnp.float32) * keep[
        :, None
    ].astype(jnp.float32)
    self_grad = lax.dot_general(
        dpre_b, w_self, (((1,), (1,)), ((), ())), preferred_element_type=jnp.float32
    )
    grad_features = (
        self_grad
        + back_sum[:rows_own]
        + jax.ops.segment_sum(returned, flat_picks, num_segments=rows_own)
    )
    total_self, total_neigh, total_bias = lax.psum(
        (term_self, term_neigh, term_bias), ("row", "col")
    )
    inv_root = 1.0 / jnp.sqrt(jnp.float32(rows_own * lax.axis_size(("row", "col"))))
    return (
        layer_out,
        grad_features,
        total_self * inv_root,
        total_neigh * inv_root,
        total_bias * inv_root,
    )


def solution(mesh):
    in_specs = (
        P(("row", "col"), None),
        P(("row", "col"), None, None),
        P(("row", "col"), None),
        P(("row", "col"), None),
        P(("row", "col"), None),
        P(("row", "col"), None, None, None),
        P(),
        P(),
        P(),
        P(("row", "col"), None),
    )
    out_specs = (P(("row", "col"), None), P(("row", "col"), None), P(), P(), P())
    return jax.shard_map(
        on_device, mesh=mesh, in_specs=in_specs, out_specs=out_specs, check_vma=False
    )
```

profile of v0, /device:TPU:0, one launch (start us, length us, event | category | flops | bytes accessed | tf_op | source)
XLA Modules:
  0.0 379.2 jit_solution(15681713276999709895)
XLA Ops:
  8.8 14.9 %gather_fusion = bf16[4096,256]{1,0:T(8,128)(2,1)S(1)} fusion(bf16[4096,256]{1,0:T(8,128)(2,1)} %param.10, s32[4096]{0:T(1024)S(1)} %broadcast_clamp_fusion), kind=kCustom, calls=%fused_computation | custom fusion | bytes 4210688 | tf_op jit(solution)/shard_map/jit(_take)/gather | solution.py:27
  26.3 7.5 %all-to-all-start = ((bf16[32,128,256]{2,1,0:T(8,128)(2,1)}), bf16[32,128,256]{2,1,0:T(8,128)(2,1)}, u32[]{:S(2)}, u32[]{:S(2)}) async-start(bf16[32,128,256]{2,1,0:T(8,128)(2,1)} %select_multiply_fusion), calls=%async_computation | async-start | bytes 4194304 | tf_op jit(solution)/shard_map/all_to_all | solution.py:8
  33.8 3.3 reduce_sum.18
  38.2 2.7 fusion.32
  40.9 42.8 %all-to-all-done = bf16[32,128,256]{2,1,0:T(8,128)(2,1)} async-done(((bf16[32,128,256]{2,1,0:T(8,128)(2,1)}), bf16[32,128,256]{2,1,0:T(8,128)(2,1)}, u32[]{:S(2)}, u32[]{:S(2)}) %all-to-all-start) | async-done | bytes 2097184 | tf_op jit(solution)/shard_map/all_to_all | solution.py:8
  83.8 3.8 %pad_maximum_fusion = bf16[8192,256]{1,0:T(8,128)(2,1)} fusion(bf16[4096,256]{1,0:T(8,128)(2,1)} %bitcast.7, bf16[4096,256]{1,0:T(8,128)(2,1)S(1)} %copy-done.2), kind=kLoop, calls=%fused_computation.13 | loop fusion | flops 8388608 | bytes 8388608 | tf_op jit(solution)/shard_map/concatenate | solution.py:29
  87.6 5.0 %gather_fusion.1 = bf16[64,128,256]{2,1,0:T(8,128)(2,1)} fusion(bf16[64,128,256]{2,1,0:T(8,128)(2,1)} %bitcast.59, s32[1024]{0:T(1024)S(1)} %pad_clamp_fusion.1), kind=kCustom, calls=%fused_computation.1 | custom fusion | bytes 8388864 | tf_op jit(solution)/shard_map/jit(_take)/gather | solution.py:35
  92.5 8.2 %fusion.10 = f32[64,128,256]{1,2,0:T(8,128)} fusion(bf16[64,128,256]{2,1,0:T(8,128)(2,1)} %gather_fusion.1, pred[64]{0:T(512)(128)(4,1)S(1)} %compare_and_fusion.2, s32[1,64,128,128]{3,2,1,0:T(8,128)} %param.15), kind=kOutput, calls=%fused_computation.27 | convolution fusion | flops 540016640 | bytes 16777280 | tf_op jit(solution)/shard_map/tij,tjf->tif/dot_general | solution.py:36
  100.7 9.0 %copy.21 = f32[64,128,256]{2,1,0:T(8,128)} copy(f32[64,128,256]{1,2,0:T(8,128)} %fusion.10) | data formatting | bytes 16777216 | tf_op jit(solution)/shard_map/tij,tjf->tif/dot_general | solution.py:36
  112.2 19.4 %scatter_fusion = f32[32,128,256]{2,1,0:T(8,128)} fusion(f32[32,128,256]{2,1,0:T(8,128)} %broadcast_in_dim.40, s32[64]{0:T(128)S(1)} %bitcast.67, f32[64,128,256]{2,1,0:T(8,128)} %copy.21), kind=kCustom, calls=%fused_computation.3 | custom fusion | flops 2097152 | bytes 25166080 | tf_op jit(solution)/shard_map/scatter-add | solution.py:37
  131.5 2.7 fusion.3
  135.7 3.4 fusion.31
  142.4 4.4 %gather_fusion.2 = bf16[64,128,256]{2,1,0:T(8,128)(2,1)} fusion(bf16[32,128,256]{2,1,0:T(8,128)(2,1)} %bitcast.58, s32[1024]{0:T(1024)S(1)} %pad_clamp_fusion), kind=kCustom, calls=%fused_computation.2 | custom fusion | bytes 8388864 | tf_op jit(solution)/shard_map/jit(_take)/gather | solution.py:63
  146.8 8.2 %fusion.13 = f32[64,128,256]{1,2,0:T(8,128)} fusion(bf16[64,128,256]{2,1,0:T(8,128)(2,1)} %gather_fusion.2, pred[64]{0:T(512)(128)(4,1)S(1)} %compare_and_fusion.1, s32[1,64,128,128]{3,2,1,0:T(8,128)} %param.15), kind=kOutput, calls=%fused_computation.28 | convolution fusion | flops 540016640 | bytes 16777280 | tf_op jit(solution)/shard_map/tij,tif->tjf/dot_general | solution.py:64
  155.0 9.0 %copy.23 = f32[64,128,256]{2,1,0:T(8,128)} copy(f32[64,128,256]{1,2,0:T(8,128)} %fusion.13) | data formatting | bytes 16777216 | tf_op jit(solution)/shard_map/tij,tif->tjf/dot_general | solution.py:64
  164.0 4.2 %broadcast_in_dim.45 = f32[64,128,256]{2,1,0:T(8,128)} broadcast(f32[]{:T(128)} %constant.24.clone.1), dimensions={} | broadcast | bytes 8388612 | tf_op jit(solution)/shard_map/broadcast_in_dim | solution.py:65
  168.3 19.8 %scatter_fusion.1 = f32[64,128,256]{2,1,0:T(8,128)} fusion(f32[64,128,256]{2,1,0:T(8,128)} %broadcast_in_dim.45, s32[64]{0:T(128)S(1)} %bitcast.68, f32[64,128,256]{2,1,0:T(8,128)} %copy.23), kind=kCustom, calls=%fused_computation.5 | custom fusion | flops 2097152 | bytes 25166080 | tf_op jit(solution)/shard_map/scatter-add | solution.py:65
  188.1 3.8 slice.23
  191.9 3.5 all-to-all-start.1
  195.6 4.8 %slice.20 = f32[32,128,256]{2,1,0:T(8,128)} slice(f32[64,128,256]{2,1,0:T(8,128)} %scatter_fusion.1), slice={[0:32], [0:128], [0:256]} | slice | bytes 8388608 | tf_op jit(solution)/shard_map/slice | solution.py:78
  203.5 5.6 %convolution_add_fusion = f32[4096,256]{1,0:T(8,128)} fusion(f32[4096,256]{1,0:T(8,128)} %bitcast.60, bf16[4096,256]{1,0:T(8,128)(2,1)} %copy-done.4, bf16[256,256]{1,0:T(8,128)(2,1)S(1)} %copy-done.8), kind=kOutput, calls=%fused_computation.8 | convolution fusion | flops 537919488 | bytes 10616832 | tf_op jit(solution)/shard_map/dot_general | solution.py:73
  209.1 57.6 %psum.23 = f32[256]{0:T(256)S(1)} all-reduce(f32[256]{0:T(256)S(1)} %get-tuple-element.17), channel_id=1, replica_groups=mesh['row'=4,'col'=8] {'row','col'}, use_global_device_ids=true, to_apply=%region_8.9 | all-reduce | flops 256 | bytes 2048 | tf_op jit(solution)/shard_map/psum | solution.py:81
  267.3 72.4 %all-reduce.3.cloned.1.call-done = (f32[256,256]{0,1:T(8,128)}, f32[256,256]{0,1:T(8,128)}) async-done(((f32[256,256]{0,1:T(8,128)}, f32[256,256]{0,1:T(8,128)}), (f32[256,256]{0,1:T(8,128)}, f32[256,256]{0,1:T(8,128)})) %all-reduce.3.cloned.1.call-update) | async-done | bytes 524304 | tf_op jit(solution)/shard_map/psum | solution.py:81
  343.3 29.0 %scatter_custom_fusion.3 = f32[4096,256]{1,0:T(8,128)} fusion(f32[4096,256]{1,0:T(8,128)} %convolution_add_fusion, s32[4096]{0:T(1024)} %bitcast.64, bf16[4096,256]{1,0:T(8,128)(2,1)} %bitcast.24, f32[4096]{0:T(1024)S(1)} %get-tuple-element.20), kind=kCustom, calls=%fused_computation.15 | custom fusion | flops 3145728 | bytes 6307840 | tf_op jit(solution)/shard_map/scatter-add | solution.py:79
  (50 shorter events, 20.1 us)
Async XLA Ops:
  7.2 127.1 %copy-start = (bf16[256,256]{1,0:T(8,128)(2,1)S(1)}, bf16[256,256]{1,0:T(8,128)(2,1)}, u32[]{:S(2)}) copy-start(bf16[256,256]{1,0:T(8,128)(2,1)} %param.17) | copy-start | bytes 393220
  26.3 10.8 %copy-start.9 = (s32[1,64]{1,0:T(1,128)S(1)}, s32[1,64]{1,0:T(1,128)}, u32[]{:S(2)}) copy-start(s32[1,64]{1,0:T(1,128)} %param.13) | copy-start | bytes 772
  26.3 11.8 %copy-start.10 = (s32[1,64]{1,0:T(1,128)S(1)}, s32[1,64]{1,0:T(1,128)}, u32[]{:S(2)}) copy-start(s32[1,64]{1,0:T(1,128)} %param.14) | copy-start | bytes 772
  26.3 11.9 %copy-start.2 = (bf16[4096,256]{1,0:T(8,128)(2,1)S(1)}, bf16[4096,256]{1,0:T(8,128)(2,1)}, u32[]{:S(2)}) copy-start(bf16[4096,256]{1,0:T(8,128)(2,1)} %param.10) | copy-start | bytes 6291460
  26.3 11.9 %copy-start.8 = (bf16[256,256]{1,0:T(8,128)(2,1)S(1)}, bf16[256,256]{1,0:T(8,128)(2,1)}, u32[]{:S(2)}) copy-start(bf16[256,256]{1,0:T(8,128)(2,1)} %param.16) | copy-start | bytes 393220
  26.3 57.5 %all-to-all-start = ((bf16[32,128,256]{2,1,0:T(8,128)(2,1)}), bf16[32,128,256]{2,1,0:T(8,128)(2,1)}, u32[]{:S(2)}, u32[]{:S(2)}) async-start(bf16[32,128,256]{2,1,0:T(8,128)(2,1)} %select_multiply_fusion), calls=%async_computation | async-start | bytes 4194304 | tf_op jit(solution)/shard_map/all_to_all | solution.py:8
  131.5 3.4 copy-start.3
  131.5 4.1 %copy-start.11 = (bf16[4096,256]{1,0:T(8,128)(2,1)S(1)}, bf16[4096,256]{1,0:T(8,128)(2,1)}, u32[]{:S(2)}) copy-start(bf16[4096,256]{1,0:T(8,128)(2,1)} %param.19) | copy-start | bytes 6291460
  131.5 4.1 %copy-start.12 = (f32[256]{0:T(256)S(1)}, f32[256]{0:T(256)}, u32[]{:S(2)}) copy-start(f32[256]{0:T(256)} %param.18) | copy-start | bytes 3076
  135.7 3.4 copy-start.6
  139.1 1.3 copy-start.4
  191.9 151.4 %all-to-all-start.1 = ((bf16[32,128,256]{2,1,0:T(8,128)(2,1)}), bf16[32,128,256]{2,1,0:T(8,128)(2,1)}, u32[]{:S(2)}, u32[]{:S(2)}) async-start(bf16[32,128,256]{2,1,0:T(8,128)(2,1)} %slice.23), calls=%async_computation.1 | async-start | bytes 4194304 | tf_op jit(solution)/shard_map/all_to_all | solution.py:12
  195.3 144.3 %all-reduce.3.cloned.1.call-start = ((), (), s32[]{:S(2)}) async-start(), calls=%async_computation.2 | async-start | bytes 1048576 | tf_op jit(solution)/shard_map/psum | solution.py:81
  195.6 4.8 %copy-start.5 = (bf16[4096,256]{1,0:T(8,128)(2,1)S(1)}, bf16[4096,256]{1,0:T(8,128)(2,1)}, u32[]{:S(2)}) copy-start(bf16[4096,256]{1,0:T(8,128)(2,1)} %copy-done.4) | copy-start | bytes 6291460
  195.6 4.8 %copy-start.7 = (bf16[4096,256]{1,0:T(8,128)(2,1)S(1)}, bf16[4096,256]{1,0:T(8,128)(2,1)}, u32[]{:S(2)}) copy-start(bf16[4096,256]{1,0:T(8,128)(2,1)} %copy-done.6) | copy-start | bytes 6291460
  339.6 32.7 %copy-start.1 = (bf16[256,256]{1,0:T(8,128)(2,1)S(1)}, bf16[256,256]{1,0:T(8,128)(2,1)}, u32[]{:S(2)}) copy-start(bf16[256,256]{1,0:T(8,128)(2,1)} %param.17) | copy-start | bytes 393220
Sparse Core Ops, SparseCore 0:
  203.7 135.9 all-reduce.2
where the time goes:
time: 380 us; the launch traced here: 379 us
  waiting for transfers between devices  115 us (30%)
  other arithmetic  85.8 us (23%)
  local copies, waits for them, and re-layouts  62 us (16%)
  blocking collectives  57.6 us (15%)
  matrix products  33.2 us (9%)
  between operations  14.2 us (4%)
  starting transfers between devices  11.2 us (3%)
    psum x1, waiting for transfers between devices, on_device(): lax.psum((term_self, term_neigh, term_bias), ('row', 'col'))  72.4 us
    psum x1, blocking collectives, on_device(): lax.psum((term_self, term_neigh, term_bias), ('row', 'col'))  57.6 us
    all_to_all x1, waiting for transfers between devices, move_rows(): lax.all_to_all(block, ('row', 'col'), split_axis=0, concat_axis=0, tiled=...  42.8 us
    scatter-add x1, other arithmetic, on_device(): jax.ops.segment_sum(returned, flat_picks, num_segments=rows_own)  29 us
    scatter-add x1, other arithmetic, on_device(): jax.ops.segment_sum(back, src, num_segments=src_blocks)  19.8 us
    scatter-add x1, other arithmetic, on_device(): jax.ops.segment_sum(prod, dst, num_segments=own_blocks)  19.4 us
    gather x1, local copies, waits for them, and re-layouts, on_device(): jnp.take(features, flat_picks, axis=0) * keep[:, None].astype(jnp.bfloat16)  14.9 us
    dot_general x1, local copies, waits for them, and re-layouts, on_device(): jnp.einsum('tij,tjf->tif', adj, picked, preferred_element_type=jnp.float32)  9 us
  transfers between devices with their start and end apart: 3, of which 2 were waited for; matrix products, arithmetic and copies ran while one was open for 7% of the time, Pallas kernels for 0%

commit v1 on v0

--- a/solution.py
+++ b/solution.py
@@ -2,6 +2,11 @@
 import jax.numpy as jnp
 from jax import lax
 from jax.sharding import PartitionSpec as P
+
+
+def one_after_other(x, first, second):
+    partial = lax.psum(x, first)
+    return lax.psum(partial, second)
 
 
 def move_rows(block):
@@ -78,8 +83,8 @@
         + back_sum[:rows_own]
         + jax.ops.segment_sum(returned, flat_picks, num_segments=rows_own)
     )
-    total_self, total_neigh, total_bias = lax.psum(
-        (term_self, term_neigh, term_bias), ("row", "col")
+    total_self, total_neigh, total_bias = one_after_other(
+        (term_self, term_neigh, term_bias), "col", "row"
     )
     inv_root = 1.0 / jnp.sqrt(jnp.float32(rows_own * lax.axis_size(("row", "col"))))
     return (

time: 380 us -> 356 us (0.937)
  waiting for transfers between devices: 115 us -> 95.7 us
    psum x1 -> x2, waiting for transfers between devices: 72.4 us -> 52.9 us  [the longest x1 41.3 us: one_after_other(): return lax.psum(partial, second)]
    psum x1 -> x2, blocking collectives: 57.6 us -> 55.4 us  [the longest x1 45 us: one_after_other(): partial = lax.psum(x, first)]
  transfers between devices with their start and end apart: 3 -> 4, of which waited for: 2 -> 3; matrix products, arithmetic and copies ran while one was open for 7% -> 6% of each run, Pallas kernels for 0% -> 0%
where the time goes in v1:
time: 356 us; the launch traced here: 355 us
  waiting for transfers between devices  95.7 us (27%)
  other arithmetic  85.8 us (24%)
  local copies, waits for them, and re-layouts  60 us (17%)
  blocking collectives  55.4 us (16%)
  matrix products  32.7 us (9%)
  between operations  14.2 us (4%)
  starting transfers between devices  11.2 us (3%)
    psum x1, blocking collectives, one_after_other(): partial = lax.psum(x, first)  45 us
    all_to_all x1, waiting for transfers between devices, move_rows(): lax.all_to_all(block, ('row', 'col'), split_axis=0, concat_axis=0, tiled=...  42.8 us
    psum x1, waiting for transfers between devices, one_after_other(): return lax.psum(partial, second)  41.3 us
    scatter-add x1, other arithmetic, on_device(): jax.ops.segment_sum(returned, flat_picks, num_segments=rows_own)  29 us
    scatter-add x1, other arithmetic, on_device(): jax.ops.segment_sum(back, src, num_segments=src_blocks)  19.8 us
    scatter-add x1, other arithmetic, on_device(): jax.ops.segment_sum(prod, dst, num_segments=own_blocks)  19.3 us
    gather x1, local copies, waits for them, and re-layouts, on_device(): jnp.take(features, flat_picks, axis=0) * keep[:, None].astype(jnp.bfloat16)  14.9 us
    psum x1, waiting for transfers between devices, one_after_other(): partial = lax.psum(x, first)  11.6 us
  transfers between devices with their start and end apart: 4, of which 3 were waited for; matrix products, arithmetic and copies ran while one was open for 6% of the time, Pallas kernels for 0%

profile of v1, /device:TPU:0, one launch (start us, length us, event | category | flops | bytes accessed | tf_op | source)
XLA Modules:
  0.0 355.1 jit_solution(8511312299684732988)
XLA Ops:
  8.8 14.9 %gather_fusion = bf16[4096,256]{1,0:T(8,128)(2,1)S(1)} fusion(bf16[4096,256]{1,0:T(8,128)(2,1)} %param.10, s32[4096]{0:T(1024)S(1)} %broadcast_clamp_fusion), kind=kCustom, calls=%fused_computation | custom fusion | bytes 4210688 | tf_op jit(solution)/shard_map/jit(_take)/gather | solution.py:32
  26.3 7.5 %all-to-all-start = ((bf16[32,128,256]{2,1,0:T(8,128)(2,1)}), bf16[32,128,256]{2,1,0:T(8,128)(2,1)}, u32[]{:S(2)}, u32[]{:S(2)}) async-start(bf16[32,128,256]{2,1,0:T(8,128)(2,1)} %select_multiply_fusion), calls=%async_computation | async-start | bytes 4194304 | tf_op jit(solution)/shard_map/all_to_all | solution.py:13
  33.8 3.3 reduce_sum.18
  40.9 42.8 %all-to-all-done = bf16[32,128,256]{2,1,0:T(8,128)(2,1)} async-done(((bf16[32,128,256]{2,1,0:T(8,128)(2,1)}), bf16[32,128,256]{2,1,0:T(8,128)(2,1)}, u32[]{:S(2)}, u32[]{:S(2)}) %all-to-all-start) | async-done | bytes 2097184 | tf_op jit(solution)/shard_map/all_to_all | solution.py:13
  83.8 3.8 %pad_maximum_fusion = bf16[8192,256]{1,0:T(8,128)(2,1)} fusion(bf16[4096,256]{1,0:T(8,128)(2,1)} %bitcast.7, bf16[4096,256]{1,0:T(8,128)(2,1)S(1)} %copy-done.2), kind=kLoop, calls=%fused_computation.13 | loop fusion | flops 8388608 | bytes 8388608 | tf_op jit(solution)/shard_map/concatenate | solution.py:34
  87.5 5.0 %gather_fusion.1 = bf16[64,128,256]{2,1,0:T(8,128)(2,1)} fusion(bf16[64,128,256]{2,1,0:T(8,128)(2,1)} %bitcast.59, s32[1024]{0:T(1024)S(1)} %pad_clamp_fusion.1), kind=kCustom, calls=%fused_computation.1 | custom fusion | bytes 8388864 | tf_op jit(solution)/shard_map/jit(_take)/gather | solution.py:40
  92.5 8.2 %fusion.10 = f32[64,128,256]{1,2,0:T(8,128)} fusion(bf16[64,128,256]{2,1,0:T(8,128)(2,1)} %gather_fusion.1, pred[64]{0:T(512)(128)(4,1)S(1)} %compare_and_fusion.2, s32[1,64,128,128]{3,2,1,0:T(8,128)} %param.15), kind=kOutput, calls=%fused_computation.27 | convolution fusion | flops 540016640 | bytes 16777280 | tf_op jit(solution)/shard_map/tij,tjf->tif/dot_general | solution.py:41
  100.7 9.0 %copy.21 = f32[64,128,256]{2,1,0:T(8,128)} copy(f32[64,128,256]{1,2,0:T(8,128)} %fusion.10) | data formatting | bytes 16777216 | tf_op jit(solution)/shard_map/tij,tjf->tif/dot_general | solution.py:41
  112.2 19.3 %scatter_fusion = f32[32,128,256]{2,1,0:T(8,128)} fusion(f32[32,128,256]{2,1,0:T(8,128)} %broadcast_in_dim.40, s32[64]{0:T(128)S(1)} %bitcast.67, f32[64,128,256]{2,1,0:T(8,128)} %copy.21), kind=kCustom, calls=%fused_computation.3 | custom fusion | flops 2097152 | bytes 25166080 | tf_op jit(solution)/shard_map/scatter-add | solution.py:42
  135.6 3.4 fusion.31
  142.4 4.4 %gather_fusion.2 = bf16[64,128,256]{2,1,0:T(8,128)(2,1)} fusion(bf16[32,128,256]{2,1,0:T(8,128)(2,1)} %bitcast.58, s32[1024]{0:T(1024)S(1)} %pad_clamp_fusion), kind=kCustom, calls=%fused_computation.2 | custom fusion | bytes 8388864 | tf_op jit(solution)/shard_map/jit(_take)/gather | solution.py:68
  146.8 8.2 %fusion.13 = f32[64,128,256]{1,2,0:T(8,128)} fusion(bf16[64,128,256]{2,1,0:T(8,128)(2,1)} %gather_fusion.2, pred[64]{0:T(512)(128)(4,1)S(1)} %compare_and_fusion.1, s32[1,64,128,128]{3,2,1,0:T(8,128)} %param.15), kind=kOutput, calls=%fused_computation.28 | convolution fusion | flops 540016640 | bytes 16777280 | tf_op jit(solution)/shard_map/tij,tif->tjf/dot_general | solution.py:69
  155.0 9.0 %copy.23 = f32[64,128,256]{2,1,0:T(8,128)} copy(f32[64,128,256]{1,2,0:T(8,128)} %fusion.13) | data formatting | bytes 16777216 | tf_op jit(solution)/shard_map/tij,tif->tjf/dot_general | solution.py:69
  164.0 4.2 %broadcast_in_dim.45 = f32[64,128,256]{2,1,0:T(8,128)} broadcast(f32[]{:T(128)} %constant.24.clone.1), dimensions={} | broadcast | bytes 8388612 | tf_op jit(solution)/shard_map/broadcast_in_dim | solution.py:70
  168.2 19.8 %scatter_fusion.1 = f32[64,128,256]{2,1,0:T(8,128)} fusion(f32[64,128,256]{2,1,0:T(8,128)} %broadcast_in_dim.45, s32[64]{0:T(128)S(1)} %bitcast.68, f32[64,128,256]{2,1,0:T(8,128)} %copy.23), kind=kCustom, calls=%fused_computation.5 | custom fusion | flops 2097152 | bytes 25166080 | tf_op jit(solution)/shard_map/scatter-add | solution.py:70
  188.0 3.8 %slice.23 = bf16[32,128,256]{2,1,0:T(8,128)(2,1)} slice(f32[64,128,256]{2,1,0:T(8,128)} %scatter_fusion.1), slice={[32:64], [0:128], [0:256]} | slice | bytes 4194304 | tf_op jit(solution)/shard_map/slice | solution.py:73
  191.8 3.5 all-to-all-start.1
  195.6 4.0 %fusion.33 = f32[256,256]{0,1:T(8,128)} fusion(bf16[4096,256]{1,0:T(8,128)(2,1)} %copy-done.7, bf16[4096,256]{1,0:T(8,128)(2,1)} %copy-done.4), kind=kOutput, calls=%fused_computation.66 | convolution fusion | flops 536870912 | bytes 4456448 | tf_op jit(solution)/shard_map/dot_general | solution.py:60
  201.1 45.0 %psum.46 = f32[256]{0:T(256)S(1)} all-reduce(f32[256]{0:T(256)S(1)} %get-tuple-element.19), channel_id=1, replica_groups=mesh['row'=4,'col'=8] {'col'}, use_global_device_ids=true, to_apply=%region_10.11 | all-reduce | flops 256 | bytes 2048 | tf_op jit(solution)/shard_map/psum | solution.py:8
  246.1 10.4 %psum.47 = f32[256]{0:T(256)S(1)} all-reduce(f32[256]{0:T(256)S(1)} %psum.46), channel_id=1, replica_groups=mesh['row'=4,'col'=8] {'row'}, use_global_device_ids=true, to_apply=%region_11.12 | all-reduce | flops 256 | bytes 2048 | tf_op jit(solution)/shard_map/psum | solution.py:9
  256.5 11.6 %all-reduce.5.cloned.1.call-done = (f32[256,256]{0,1:T(8,128)}, f32[256,256]{0,1:T(8,128)}) async-done(((f32[256,256]{0,1:T(8,128)}, f32[256,256]{0,1:T(8,128)}), (f32[256,256]{0,1:T(8,128)}, f32[256,256]{0,1:T(8,128)})) %all-reduce.5.cloned.1.call-update) | async-done | bytes 524304 | tf_op jit(solution)/shard_map/psum | solution.py:8
  271.6 2.8 convolution_add_fusion
  274.3 41.3 %all-reduce.7.cloned.1.call-done = (f32[256,256]{0,1:T(8,128)}, f32[256,256]{0,1:T(8,128)}) async-done(((f32[256,256]{0,1:T(8,128)}, f32[256,256]{0,1:T(8,128)}), (f32[256,256]{0,1:T(8,128)}, f32[256,256]{0,1:T(8,128)})) %all-reduce.7.cloned.1.call-update) | async-done | bytes 524304 | tf_op jit(solution)/shard_map/psum | solution.py:9
  319.3 29.0 %scatter_custom_fusion.3 = f32[4096,256]{1,0:T(8,128)} fusion(f32[4096,256]{1,0:T(8,128)} %convolution_add_fusion, s32[4096]{0:T(1024)} %bitcast.64, bf16[4096,256]{1,0:T(8,128)(2,1)} %bitcast.24, f32[4096]{0:T(1024)S(1)} %get-tuple-element.22), kind=kCustom, calls=%fused_computation.15 | custom fusion | flops 3145728 | bytes 6307840 | tf_op jit(solution)/shard_map/scatter-add | solution.py:84
  (54 shorter events, 26.8 us)
Async XLA Ops:
  7.2 127.1 %copy-start = (bf16[256,256]{1,0:T(8,128)(2,1)S(1)}, bf16[256,256]{1,0:T(8,128)(2,1)}, u32[]{:S(2)}) copy-start(bf16[256,256]{1,0:T(8,128)(2,1)} %param.17) | copy-start | bytes 393220
  26.3 10.8 %copy-start.9 = (s32[1,64]{1,0:T(1,128)S(1)}, s32[1,64]{1,0:T(1,128)}, u32[]{:S(2)}) copy-start(s32[1,64]{1,0:T(1,128)} %param.13) | copy-start | bytes 772
  26.3 11.8 %copy-start.10 = (s32[1,64]{1,0:T(1,128)S(1)}, s32[1,64]{1,0:T(1,128)}, u32[]{:S(2)}) copy-start(s32[1,64]{1,0:T(1,128)} %param.14) | copy-start | bytes 772
  26.3 11.9 %copy-start.2 = (bf16[4096,256]{1,0:T(8,128)(2,1)S(1)}, bf16[4096,256]{1,0:T(8,128)(2,1)}, u32[]{:S(2)}) copy-start(bf16[4096,256]{1,0:T(8,128)(2,1)} %param.10) | copy-start | bytes 6291460
  26.3 11.9 %copy-start.8 = (bf16[256,256]{1,0:T(8,128)(2,1)S(1)}, bf16[256,256]{1,0:T(8,128)(2,1)}, u32[]{:S(2)}) copy-start(bf16[256,256]{1,0:T(8,128)(2,1)} %param.16) | copy-start | bytes 393220
  26.3 57.5 %all-to-all-start = ((bf16[32,128,256]{2,1,0:T(8,128)(2,1)}), bf16[32,128,256]{2,1,0:T(8,128)(2,1)}, u32[]{:S(2)}, u32[]{:S(2)}) async-start(bf16[32,128,256]{2,1,0:T(8,128)(2,1)} %select_multiply_fusion), calls=%async_computation | async-start | bytes 4194304 | tf_op jit(solution)/shard_map/all_to_all | solution.py:13
  131.5 3.4 copy-start.3
  131.5 4.1 %copy-start.11 = (bf16[4096,256]{1,0:T(8,128)(2,1)S(1)}, bf16[4096,256]{1,0:T(8,128)(2,1)}, u32[]{:S(2)}) copy-start(bf16[4096,256]{1,0:T(8,128)(2,1)} %param.19) | copy-start | bytes 6291460
  131.5 4.1 %copy-start.12 = (f32[256]{0:T(256)S(1)}, f32[256]{0:T(256)}, u32[]{:S(2)}) copy-start(f32[256]{0:T(256)} %param.18) | copy-start | bytes 3076
  135.6 3.4 copy-start.7
  139.0 1.4 copy-start.4
  191.8 127.4 %all-to-all-start.1 = ((bf16[32,128,256]{2,1,0:T(8,128)(2,1)}), bf16[32,128,256]{2,1,0:T(8,128)(2,1)}, u32[]{:S(2)}, u32[]{:S(2)}) async-start(bf16[32,128,256]{2,1,0:T(8,128)(2,1)} %slice.23), calls=%async_computation.1 | async-start | bytes 4194304 | tf_op jit(solution)/shard_map/all_to_all | solution.py:17
  195.3 72.8 %all-reduce.5.cloned.1.call-start = ((), (), s32[]{:S(2)}) async-start(), calls=%async_computation.2 | async-start | bytes 1048576 | tf_op jit(solution)/shard_map/psum | solution.py:8
  195.6 4.0 %copy-start.5 = (bf16[4096,256]{1,0:T(8,128)(2,1)S(1)}, bf16[4096,256]{1,0:T(8,128)(2,1)}, u32[]{:S(2)}) copy-start(bf16[4096,256]{1,0:T(8,128)(2,1)} %copy-done.4) | copy-start | bytes 6291460
  201.1 114.5 %all-reduce.7.cloned.1.call-start = ((), (), s32[]{:S(2)}) async-start(), calls=%async_computation.3 | async-start | bytes 1048576 | tf_op jit(solution)/shard_map/psum | solution.py:9
  268.7 2.9 copy-start.6
  315.6 32.7 %copy-start.1 = (bf16[256,256]{1,0:T(8,128)(2,1)S(1)}, bf16[256,256]{1,0:T(8,128)(2,1)}, u32[]{:S(2)}) copy-start(bf16[256,256]{1,0:T(8,128)(2,1)} %param.17) | copy-start | bytes 393220
Sparse Core Ops, SparseCore 0:
  201.2 66.8 all-reduce.4
  271.1 44.4 all-reduce.6
